TPU v7x, 256 devices: a whole 4x4x8 slice. The times are simulated.
256 devices in a mesh: cp: 64 (over y_lo, x, z), tp: 4 (over y_hi, core).
Axes of the slice: x: 4, y: 4 (y_hi: 2, y_lo: 2; y = y_hi * 2 + y_lo), z: 8, core: 2. Of those that a mesh axis runs over, the one named last changes fastest.
Arguments:
- queries: bfloat16 [12288, 2048], P('cp', 'tp'), may hold values from -128 to 128
- keys: bfloat16 [12288, 256], P('cp'), may hold values from -6 to 6
- values: bfloat16 [12288, 256], P('cp'), may hold values from -6 to 6
- positions: int32 [12288], replicated, may hold values from 0 to 12287, as said below
- out_weight: bfloat16 [2048, 8192], P('tp'), may hold values from -0.125 to 0.125
Outputs:
- mixed: bfloat16 [12288, 8192], P(('cp', 'tp'))
Inputs may be any that keep to these rules, and one draw needn't show every extreme that they name: positions is a permutation of 0 to 12287. The tokens stored at indices d * 192 to (d + 1) * 192 - 1 form two runs of 96 consecutive positions, the first starting at b * 96 and the second at (127 - b) * 96 for some b, each b used by one d.
All inputs are finite; a program needn't handle non-finite values.
Results may differ from a plain program's by a relative error of at most 0.013.
Values may be sent and summed in bfloat16 or wider, within the bound.
A program may use at most 128 MiB of HBM per device.

v0:
```python
import jax
import jax.numpy as jnp
from jax import lax
from jax.sharding import PartitionSpec as P

HEAD = 128
GROUP = 8


def sent_together(arrays, axis, dim, along):
    both = jnp.concatenate(arrays, axis=along)
    result, at, outs = (lax.all_gather(both, axis, axis=dim, tiled=True), 0, [])
    for a in arrays:
        outs.append(lax.slice_in_dim(result, at, at + a.shape[along], axis=along))
        at += a.shape[along]
    return tuple(outs)


def shards(queries, keys, values, positions, out_weight):
    tok_rows = queries.shape[0]
    head_count = queries.shape[1] // HEAD
    score_scale = HEAD ** (-0.5)
    kv_group = lax.axis_index("tp") * head_count // GROUP
    own_keys = lax.dynamic_slice_in_dim(keys, kv_group * HEAD, HEAD, 1)
    own_values = lax.dynamic_slice_in_dim(values, kv_group * HEAD, HEAD, 1)
    query_pos = lax.dynamic_slice_in_dim(positions, lax.axis_index("cp") * tok_rows, tok_rows, 0)
    local_queries = queries.reshape(tok_rows, head_count, HEAD)
    run_max = jnp.full((tok_rows, head_count), -1e30, jnp.float32)
    arrived_keys, arrived_values = sent_together((own_keys, own_values), "cp", 0, 1)
    allowed = (positions[None, :] <= query_pos[:, None])[:, None, :]
    scores = (
        jnp.einsum("qhd,kd->qhk", local_queries, arrived_keys, preferred_element_type=jnp.float32)
        * score_scale
    )
    scores = jnp.where(allowed, scores, -1e30)
    new_max = jnp.maximum(run_max, jnp.max(scores, axis=-1))
    weights = jnp.where(allowed, jnp.exp(scores - new_max[:, :, None]), 0.0)
    run_sum = jnp.sum(weights, axis=-1)
    run_out = jnp.einsum(
        "qhk,kd->qhd",
        weights.astype(jnp.bfloat16),
        arrived_values,
        preferred_element_type=jnp.float32,
    )
    final_state = (new_max, run_sum, run_out)
    run_max, run_sum, run_out = final_state
    attended = (
        (run_out / run_sum[:, :, None]).astype(jnp.bfloat16).reshape(tok_rows, head_count * HEAD)
    )
    return lax.psum_scatter(
        jnp.dot(attended, out_weight, preferred_element_type=jnp.float32).astype(jnp.bfloat16),
        "tp",
        scatter_dimension=0,
        tiled=True,
    )


def solution(mesh):
    in_specs = (P("cp", "tp"), P("cp", None), P("cp", None), P(), P("tp", None))
    out_specs = P(("cp", "tp"), None)
    return jax.shard_map(shards, mesh=mesh, in_specs=in_specs, out_specs=out_specs, check_vma=False)
```

profile of v0, /device:TPU:1, one launch (start us, length us, event | category | flops | bytes accessed | tf_op | source)
XLA Modules:
  0.0 435.2 jit_solution(11407416021522625930)
XLA Ops:
  6.5 0.0 copy-start
  6.5 0.0 all-gather.2.cloned.1.call-start
  6.5 0.9 constant_dynamic-slice_fusion
  7.4 0.7 pad_maximum_fusion
  8.1 0.0 all-gather.2.cloned.1.call-update
  8.1 0.0 reduce-scatter.2.cloned.1.call-start
  8.1 0.8 dynamic_slice.9
  8.9 2.2 broadcast_compare_fusion
  11.1 264.4 %all-gather.2.cloned.1.call-done = bf16[12288,256]{1,0:T(8,128)(2,1)} async-done(((bf16[192,256]{1,0:T(8,128)(2,1)}), bf16[12288,256]{1,0:T(8,128)(2,1)}) %all-gather.2.cloned.1.call-update) | async-done | bytes 6291472 | tf_op jit(solution)/shard_map/all_gather | solution.py:12
  275.5 0.0 copy-done
  275.5 17.9 %fusion = (f32[192,4]{0,1:T(4,128)S(1)}, f32[12288,192,4]{0,1,2:T(8,128)}) fusion(pred[192,12288]{1,0:T(8,128)(4,1)S(1)} %broadcast_compare_fusion, bf16[12288,256]{1,0:T(8,128)(2,1)} %all-gather.2.cloned.1.call-done, bf16[192,512]{1,0:T(8,128)(2,1)S(1)} %copy-done), kind=kOutput, calls=%fused_computation.2 | convolution fusion | flops 2444229888 | bytes 43453440 | tf_op jit(solution)/shard_map/qhd,kd->qhk/dot_general | solution.py:32
  293.4 18.1 %fusion.1 = f32[192,4]{0,1:T(4,128)S(1)} fusion(f32[12288,192,4]{0,1,2:T(8,128)} %get-tuple-element.6, f32[192,4]{0,1:T(4,128)S(1)} %broadcast_maximum_fusion, pred[192,12288]{1,0:T(8,128)(4,1)S(1)} %broadcast_compare_fusion), kind=kLoop, calls=%fused_computation.3 | loop fusion | flops 47185152 | bytes 40114176 | tf_op jit(solution)/shard_map/reduce_sum | solution.py:38
  311.5 17.7 %fusion.13 = bf16[4,24,8,128]{3,2,1,0:T(8,128)(2,1)S(1)} fusion(bf16[12288,256]{1,0:T(8,128)(2,1)} %all-gather.2.cloned.1.call-done, f32[12288,192,4]{0,1,2:T(8,128)} %get-tuple-element.6, f32[192,4]{0,1:T(4,128)S(1)} %broadcast_maximum_fusion, pred[192,12288]{1,0:T(8,128)(4,1)S(1)} %broadcast_compare_fusion, f32[192,4]{0,1:T(4,128)S(1)} %fusion.1), kind=kOutput, calls=%fused_computation.14 | convolution fusion | flops 2463301632 | bytes 43456512 | tf_op jit(solution)/shard_map/qhk,kd->qhd/dot_general | solution.py:39
  329.3 6.9 %convolution_convert_fusion = bf16[192,8192]{1,0:T(8,128)(2,1)} fusion(bf16[512,8192]{1,0:T(8,128)(2,1)} %param.9, bf16[4,24,8,128]{3,2,1,0:T(8,128)(2,1)S(1)} %fusion.13), kind=kOutput, calls=%fused_computation.7 | convolution fusion | flops 1612185600 | bytes 11730944 | tf_op jit(solution)/shard_map/dot_general | solution.py:51
  336.2 0.0 reduce-scatter.2.cloned.1.call-update
  336.2 92.1 %reduce-scatter.2.cloned.1.call-done = bf16[48,8192]{1,0:T(8,128)(2,1)} async-done(((bf16[192,8192]{1,0:T(8,128)(2,1)}), bf16[48,8192]{1,0:T(8,128)(2,1)}) %reduce-scatter.2.cloned.1.call-update) | async-done | bytes 786448 | tf_op jit(solution)/shard_map/reduce_scatter | solution.py:50
  (1 shorter events, 0.0 us)
Async XLA Ops:
  6.5 269.0 %copy-start = (bf16[192,512]{1,0:T(8,128)(2,1)S(1)}, bf16[192,512]{1,0:T(8,128)(2,1)}, u32[]{:S(2)}) copy-start(bf16[192,512]{1,0:T(8,128)(2,1)} %param.5) | copy-start | bytes 589828
  6.5 269.0 %all-gather.2.cloned.1.call-start = ((), (), s32[]{:S(2)}) async-start(), calls=%async_computation.1 | async-start | bytes 6389760 | tf_op jit(solution)/shard_map/all_gather | solution.py:12
  8.1 420.2 %reduce-scatter.2.cloned.1.call-start = ((), (), s32[]{:S(2)}) async-start(), calls=%async_computation.2 | async-start | bytes 3932160 | tf_op jit(solution)/shard_map/reduce_scatter | solution.py:50
Sparse Core Ops, SparseCore 0:
  9.1 266.3 all-gather.1
  336.4 91.9 reduce-scatter.1
where the time goes:
time: 436 us; the launch traced here: 435 us
  waiting for transfers between devices  357 us (82%)
  matrix products  42.6 us (10%)
  other arithmetic  20.9 us (5%)
  between operations  13.4 us (3%)
    all_gather x1, waiting for transfers between devices, sent_together(): result, at, outs = (lax.all_gather(both, axis, axis=dim, tiled=True), 0, [])  264 us
    reduce_scatter x1, waiting for transfers between devices, shards(): lax.psum_scatter(jnp.dot(attended, out_weight, preferred_element_type=jnp...  92.1 us
    reduce_sum x1, other arithmetic, shards(): run_sum = jnp.sum(weights, axis=-1)  18.1 us
    dot_general x1, matrix products, shards(): jnp.einsum('qhd,kd->qhk', local_queries, arrived_keys, preferred_element_...  17.9 us
    dot_general x1, matrix products, shards(): jnp.einsum('qhk,kd->qhd', weights.astype(jnp.bfloat16), arrived_values, p...  17.7 us
  transfers between devices with their start and end apart: 2, of which 2 were waited for; matrix products, arithmetic and copies ran while one was open for 1% of the time, Pallas kernels for 0%

commit v1 on v0

v1 whole, which is shorter than its diff:
```python
import functools
import math

import jax
import jax.numpy as jnp
from jax import lax
from jax.experimental import pallas as pl
from jax.experimental.pallas import tpu as pltpu
from jax.sharding import PartitionSpec as P

MESH = pl.DeviceIdType.MESH
HEAD = 128
GROUP = 8
NY, NX, NZ = 2, 4, 8
NCP = NY * NX * NZ
RUN = 96
TOK = 192
HEADS = 4
ROWS = RUN * HEADS
NCOL = 8192
HALF = NCOL // 2
NJ = 8
CW = HALF // NJ
SCALE = HEAD ** (-0.5) * math.log2(math.e)
NEG = -1e30


def kernel(q_ref, k_ref, v_ref, pos_ref, w_ref, out_ref,
           kv, own_kv, qv, q2t, acc_l, acc_h, sum_l, sum_h, max_l, max_h,
           att, wbuf, pbuf, relay, rbuf, lbuf, obuf, pos,
           fill_sem, in_sem, w_sem, ag_send, ag_recv, dd_send, dd_recv,
           att_sem, rs_send, rs_recv, fw_send, fw_recv, lo_send, lo_recv, out_sem):
    cp = lax.axis_index("cp")
    tp = lax.axis_index("tp")
    core = tp % 2
    yh = tp // 2
    z = cp % NZ
    x = (cp // NZ) % NX
    y = cp // (NZ * NX)

    def cp_of(yy, xx, zz):
        return (yy * NX + xx) * NZ + zz

    partner = dict(cp=cp, tp=yh * 2 + 1 - core)

    def at_z(k):
        return dict(cp=cp_of(y, x, (z + k + NZ) % NZ), tp=tp)

    def at_x(k):
        return dict(cp=cp_of(y, (x + k + NX) % NX, z), tp=tp)

    flip = dict(cp=cp_of(1 - y, x, z), tp=tp)

    def ring_y(sign, e):
        yy = (yh * 2 + y + sign + 4) % 4
        return dict(cp=cp_of(yy % 2, x, z), tp=(yy // 2) * 2 + e)

    q_copy = pltpu.make_async_copy(q_ref, qv, in_sem.at[0])
    q_copy.start()
    pos_copy = pltpu.make_async_copy(pos_ref, pos, in_sem.at[1])
    pos_copy.start()
    slot_a = z * 8 + x * 2 + y
    slot_b = x * 16 + z * 2 + y
    slot_d = y * 32 + x * 8 + z
    own_slots = (slot_a, slot_b, slot_d)
    fills = []
    cols = pl.ds(pl.multiple_of(yh * HEAD, HEAD), HEAD)
    for f in range(3):
        for h in range(2):
            for src, kind in ((k_ref, 0), (v_ref, 2)):
                rows = pl.ds(pl.multiple_of(h * RUN + 32 * f + 16 * core, 16), 16)
                fills.append(pltpu.make_async_copy(
                    src.at[rows, cols], kv.at[f, core, own_slots[f], kind + h], fill_sem.at[len(fills)]))
    own_fills = []
    for h in range(2):
        for src, kind in ((k_ref, 0), (v_ref, 2)):
            own_fills.append(pltpu.make_async_copy(
                src.at[pl.ds(h * RUN, RUN), cols], own_kv.at[kind + h], fill_sem.at[12 + len(own_fills)]))
    for c in fills + own_fills:
        c.start()

    barrier = pltpu.get_barrier_semaphore()
    peers = [at_z(k) for k in range(1, NZ)] + [at_x(k) for k in range(1, NX)] + [partner]
    peers += [ring_y(s, e) for s in (1, -1) for e in (0, 1)]
    for p in peers:
        pl.semaphore_signal(barrier, inc=1, device_id=p, device_id_type=MESH)
    pl.semaphore_wait(barrier, len(peers))
    for c in fills:
        c.wait()

    sends = []

    def rcopy(src, dst, ssem, rsem, dev):
        return pltpu.make_async_remote_copy(src_ref=src, dst_ref=dst, send_sem=ssem, recv_sem=rsem,
                                            device_id=dev, device_id_type=MESH)

    def gather(f, slot, n, sem, dev):
        ref = kv.at[f, core, pl.ds(slot, n)]
        c = rcopy(ref, ref, ag_send.at[sem], ag_recv.at[sem], dev)
        c.start()
        sends.append(c)

    def arrive(f, slot, n, sem):
        ref = kv.at[f, core, pl.ds(slot, n)]
        rcopy(ref, ref, ag_send.at[sem], ag_recv.at[sem], partner).wait_recv()

    def share(f, slot, n, sem):
        ref = kv.at[f, core, pl.ds(slot, n)]
        c = rcopy(ref, ref, dd_send.at[sem], dd_recv.at[sem], partner)
        c.start()
        sends.append(c)

    def shared(f, slot, n, sem):
        ref = kv.at[f, 1 - core, pl.ds(slot, n)]
        rcopy(ref, ref, dd_send.at[sem], dd_recv.at[sem], partner).wait_recv()

    def zz(k):
        return (z + k + NZ) % NZ

    def xx(k):
        return (x + k + NX) % NX

    sem_ids = {}

    def sid(*key):
        return sem_ids.setdefault(key, len(sem_ids))

    gather(0, slot_a, 1, sid("a.y"), flip)
    gather(1, slot_b, 1, sid("b.y"), flip)
    for k in (1, -1, 2, -2, 3, -3, 4):
        gather(2, slot_d, 1, sid("d.z", -k if k != 4 else 4), at_z(k))

    my_rows = pl.ds(pl.multiple_of(core * 512, 512), 512)
    w_own = pltpu.make_async_copy(
        w_ref.at[:, pl.ds(pl.multiple_of(core * HALF, HALF), HALF)], wbuf.at[my_rows], w_sem.at[0])
    w_own.start()
    w_far = rcopy(w_ref.at[:, pl.ds(pl.multiple_of((1 - core) * HALF, HALF), HALF)], wbuf.at[my_rows],
                  w_sem.at[1], w_sem.at[2], partner)
    w_far.start()
    other_rows = pl.ds(pl.multiple_of((1 - core) * 512, 512), 512)
    w_in = rcopy(w_ref.at[:, pl.ds(0, HALF)], wbuf.at[other_rows], w_sem.at[1], w_sem.at[2], partner)

    arrive(0, z * 8 + x * 2 + 1 - y, 1, sid("a.y"))
    for k in (1, -1, 2):
        gather(0, z * 8 + x * 2, 2, sid("a.x", -k if k != 2 else 2), at_x(k))
    arrive(1, x * 16 + z * 2 + 1 - y, 1, sid("b.y"))

    def send_b_z(k, sign):
        gather(1, x * 16 + zz(-sign * k) * 2, 2, sid("b.z", sign, k + 1), at_z(sign))

    def send_b_x(k):
        slot = x * 16 + zz(k) * 2
        gather(1, slot, 2, sid("b.x", k % NZ, 1), at_x(1))
        gather(1, slot, 2, sid("b.x", k % NZ, -1), at_x(-1))

    def relay_b_x(k):
        zk = zz(k)
        arrive(1, xx(-1) * 16 + zk * 2, 2, sid("b.x", k % NZ, 1))
        if k % 2 == 0:
            gather(1, xx(-1) * 16 + zk * 2, 2, sid("b.x", k % NZ, 2), at_x(1))
        arrive(1, xx(1) * 16 + zk * 2, 2, sid("b.x", k % NZ, -1))
        if k % 2 == 1:
            gather(1, xx(1) * 16 + zk * 2, 2, sid("b.x", k % NZ, 2), at_x(-1))

    def last_b_x(k):
        arrive(1, xx(2) * 16 + zz(k) * 2, 2, sid("b.x", k % NZ, 2))

    def arrive_b_z(k, sign):
        arrive(1, x * 16 + zz(-sign * k) * 2, 2, sid("b.z", sign, k))

    STEPS = {1: 4, -1: 3}

    send_b_z(0, 1)
    send_b_z(0, -1)
    send_b_x(0)

    for k in (1, -1, 2):
        arrive(0, z * 8 + xx(k) * 2, 2, sid("a.x", k))
    A_STEPS = {(0, 1): 4, (0, -1): 3, (1, 1): 3, (1, -1): 4}

    def send_a_z(k, sign, piece):
        gather(0, zz(-sign * k) * 8 + piece * 4, 4, sid("a.z", piece, sign, k + 1), at_z(sign))

    def arrive_a_z(k, sign, piece):
        arrive(0, zz(-sign * k) * 8 + piece * 4, 4, sid("a.z", piece, sign, k))

    for piece in (0, 1):
        for sign in (1, -1):
            send_a_z(0, sign, piece)
    share(0, z * 8, 8, 0)

    for k in (1, -1, 2, -2, 3, -3, 4):
        arrive(2, y * 32 + x * 8 + zz(k), 1, sid("d.z", k))
    own_line = y * 32 + x * 8
    gather(2, own_line, 8, sid("d.x", 1), at_x(1))
    gather(2, own_line, 8, sid("d.x", -1), at_x(-1))
    gather(2, own_line, 8, sid("d.y", 0), flip)
    share(2, own_line, 8, 16)

    def flow_a(k):
        for piece in (0, 1):
            for sign in (1, -1):
                last = A_STEPS[piece, sign]
                if k <= last:
                    arrive_a_z(k, sign, piece)
                    if k < last:
                        send_a_z(k, sign, piece)
        if k < 4:
            share(0, zz(k) * 8, 8, k)
            share(0, zz(-k) * 8, 8, 8 - k)
        else:
            share(0, zz(4) * 8, 8, 4)

    def flow_b(k):
        for sign in (1, -1):
            if k <= STEPS[sign]:
                arrive_b_z(k, sign)
                if k < STEPS[sign]:
                    send_b_z(k, sign)
                send_b_x(-sign * k)

    flow_b(1)
    relay_b_x(0)
    flow_a(1)
    flow_b(2)
    relay_b_x(1)
    relay_b_x(-1)
    arrive(2, y * 32 + xx(-1) * 8, 8, sid("d.x", 1))
    gather(2, y * 32 + xx(-1) * 8, 4, sid("d.x2", 0), at_x(1))
    gather(2, y * 32 + xx(-1) * 8, 8, sid("d.y", -1), flip)
    share(2, y * 32 + xx(-1) * 8, 8, 17)
    arrive(2, y * 32 + xx(1) * 8, 8, sid("d.x", -1))
    gather(2, y * 32 + xx(1) * 8 + 4, 4, sid("d.x2", 1), at_x(-1))
    gather(2, y * 32 + xx(1) * 8, 8, sid("d.y", 1), flip)
    share(2, y * 32 + xx(1) * 8, 8, 18)
    flow_a(2)
    flow_b(3)
    relay_b_x(2)
    relay_b_x(-2)
    arrive(2, y * 32 + xx(2) * 8, 4, sid("d.x2", 0))
    arrive(2, y * 32 + xx(2) * 8 + 4, 4, sid("d.x2", 1))
    gather(2, y * 32 + xx(2) * 8, 8, sid("d.y", 2), flip)
    share(2, y * 32 + xx(2) * 8, 8, 19)
    flow_b(4)
    share(1, x * 16, 16, 8)
    flow_a(3)
    relay_b_x(3)
    relay_b_x(-3)
    relay_b_x(4)
    share(1, xx(-1) * 16, 16, 9)
    share(1, xx(1) * 16, 16, 10)
    arrive(2, (1 - y) * 32 + x * 8, 8, sid("d.y", 0))
    share(2, (1 - y) * 32 + x * 8, 8, 20)
    for k in (-1, 1):
        arrive(2, (1 - y) * 32 + xx(k) * 8, 8, sid("d.y", k))
        share(2, (1 - y) * 32 + xx(k) * 8, 8, 22 + k)
    flow_a(4)
    for k in (0, 1, -1, 2, -2, 3, -3, 4):
        last_b_x(k)
    share(1, xx(2) * 16, 16, 11)
    arrive(2, (1 - y) * 32 + xx(2) * 8, 8, sid("d.y", 2))
    share(2, (1 - y) * 32 + xx(2) * 8, 8, 22)

    assert len(sem_ids) == N_AG

    q_copy.wait()
    pos_copy.wait()
    own0 = pos[cp * TOK]
    own1 = pos[cp * TOK + RUN]
    own_first = own0 < own1
    own_low = jnp.minimum(own0, own1)

    qa = jnp.concatenate([qv[0:RUN, h * HEAD:(h + 1) * HEAD] for h in range(HEADS)], axis=0)
    qb = jnp.concatenate([qv[RUN:TOK, h * HEAD:(h + 1) * HEAD] for h in range(HEADS)], axis=0)
    q2t[0:HEAD, :] = jnp.where(own_first, qa, qb).T
    q2t[HEAD:2 * HEAD, :] = jnp.where(own_first, qb, qa).T

    TN = (((0,), (0,)), ((), ()))

    for c in own_fills:
        c.wait()

    lane = lax.broadcasted_iota(jnp.int32, (RUN, ROWS), 1)
    keep = lax.broadcasted_iota(jnp.int32, (RUN, ROWS), 0) <= lane % RUN

    def triangle(kk, vv, qt, acc, total, top):
        s = jnp.dot(kk, qt, preferred_element_type=jnp.float32)
        s = jnp.where(keep, s, NEG)
        m = jnp.max(s, axis=0, keepdims=True)
        p = jnp.exp2(s * SCALE - m * SCALE)
        top[...] = m
        total[...] = jnp.sum(p.reshape(RUN // 8, 8, ROWS), axis=0)
        acc[...] = lax.dot_general(vv, p.astype(jnp.bfloat16), TN, preferred_element_type=jnp.float32)

    k0, k1, v0, v1 = (own_kv[i] for i in range(4))
    triangle(jnp.where(own_first, k0, k1), jnp.where(own_first, v0, v1), q2t[0:HEAD, :], acc_l, sum_l, max_l)
    triangle(jnp.where(own_first, k1, k0), jnp.where(own_first, v1, v0), q2t[HEAD:2 * HEAD, :], acc_h, sum_h, max_h)

    zero = jnp.zeros((16, HEAD), jnp.bfloat16)

    def chunk(f, i):
        low_f, high_f = [], []
        kl, vl, ka, kb, va, vb = [], [], [], [], [], []
        for j in range(8):
            s_z = jnp.where(f == 0, i, jnp.where(f == 1, (i % 2) * 4 + j // 2, j))
            s_x = jnp.where(f == 0, j // 2, jnp.where(f == 1, i // 2, i % 4))
            s_y = jnp.where(f == 2, i // 4, j % 2)
            s = cp_of(s_y, s_x, s_z)
            p0 = pos[s * TOK]
            p1 = pos[s * TOK + RUN]
            first = p0 < p1
            low = jnp.minimum(p0, p1) < own_low
            high = jnp.minimum(p0, p1) > own_low
            low_f.append(low)
            high_f.append(high)
            for c in range(2):
                t0, t1, u0, u1 = (kv[f, c, i * 8 + j, n] for n in range(4))
                kl_ = jnp.where(first, t0, t1)
                vl_ = jnp.where(first, u0, u1)
                kl.append(kl_)
                vl.append(vl_)
                ka.append(jnp.where(low, kl_, zero))
                va.append(jnp.where(low, vl_, zero))
                kb.append(jnp.where(high, jnp.where(first, t1, t0), zero))
                vb.append(jnp.where(high, jnp.where(first, u1, u0), zero))
        cat = functools.partial(jnp.concatenate, axis=0)
        k2 = jnp.concatenate([cat(ka), cat(kb)], axis=1)
        v2 = jnp.concatenate([cat(va), cat(vb)], axis=1)
        s1 = jnp.dot(cat(kl), q2t[HEAD:2 * HEAD, :], preferred_element_type=jnp.float32)
        s2 = jnp.dot(k2, q2t[...], preferred_element_type=jnp.float32)
        m_h = jnp.max(s1.reshape(32, 8, ROWS), axis=0)
        m_l = jnp.full((8, ROWS), NEG, jnp.float32)
        for j in range(8):
            t = jnp.max(s2[32 * j:32 * j + 32].reshape(4, 8, ROWS), axis=0)
            m_l = jnp.maximum(m_l, jnp.where(low_f[j], t, NEG))
            m_h = jnp.maximum(m_h, jnp.where(high_f[j], t, NEG))
        old_l, old_h = max_l[...], max_h[...]
        new_l = jnp.maximum(old_l, jnp.max(m_l, axis=0, keepdims=True))
        new_h = jnp.maximum(old_h, jnp.max(m_h, axis=0, keepdims=True))
        fade_l = jnp.exp2((old_l - new_l) * SCALE)
        fade_h = jnp.exp2((old_h - new_h) * SCALE)
        max_l[...] = new_l
        max_h[...] = new_h
        at_l = jnp.broadcast_to(new_l * SCALE, (8, ROWS))
        at_h = jnp.broadcast_to(new_h * SCALE, (8, ROWS))
        p1 = jnp.exp2(s1.reshape(32, 8, ROWS) * SCALE - at_h[None])
        t_h = sum_h[...] * fade_h + jnp.sum(p1, axis=0)
        t_l = sum_l[...] * fade_l
        p2 = []
        for j in range(8):
            m = jnp.where(low_f[j], at_l, jnp.where(high_f[j], at_h, -NEG))
            p = jnp.exp2(s2[32 * j:32 * j + 32].reshape(4, 8, ROWS) * SCALE - m[None])
            t = jnp.sum(p, axis=0)
            t_l = t_l + jnp.where(low_f[j], t, 0.0)
            t_h = t_h + jnp.where(high_f[j], t, 0.0)
            p2.append(p.reshape(32, ROWS))
        sum_l[...] = t_l
        sum_h[...] = t_h
        r1 = lax.dot_general(cat(vl), p1.reshape(256, ROWS).astype(jnp.bfloat16), TN,
                             preferred_element_type=jnp.float32)
        r2 = lax.dot_general(v2, cat(p2).astype(jnp.bfloat16), TN, preferred_element_type=jnp.float32)
        acc_l[...] = acc_l[...] * fade_l + r2[0:HEAD]
        acc_h[...] = acc_h[...] * fade_h + (r1 + r2[HEAD:2 * HEAD])

    for i in range(8):
        shared(0, zz(i) * 8, 8, i)
    for n, k in enumerate((0, -1, 1, 2)):
        shared(1, xx(k) * 16, 16, 8 + n)
    for n, k in enumerate((0, -1, 1, 2)):
        shared(2, y * 32 + xx(k) * 8, 8, 16 + n)
    for n, k in ((20, 0), (21, -1), (23, 1), (22, 2)):
        shared(2, (1 - y) * 32 + xx(k) * 8, 8, n)

    def rounds(r, carry):
        chunk(r // 8, r % 8)
        return carry

    lax.fori_loop(0, 24, rounds, 0)

    fin_l = acc_l[...] / jnp.sum(sum_l[...], axis=0, keepdims=True)
    fin_h = acc_h[...] / jnp.sum(sum_h[...], axis=0, keepdims=True)
    fin_a = jnp.where(own_first, fin_l, fin_h).T.astype(jnp.bfloat16)
    fin_b = jnp.where(own_first, fin_h, fin_l).T.astype(jnp.bfloat16)
    for h in range(HEADS):
        att[core, 0:RUN, h * HEAD:(h + 1) * HEAD] = fin_a[h * RUN:(h + 1) * RUN]
        att[core, RUN:TOK, h * HEAD:(h + 1) * HEAD] = fin_b[h * RUN:(h + 1) * RUN]
    att_copy = rcopy(att.at[core], att.at[core], att_sem.at[0], att_sem.at[1], partner)
    att_copy.start()
    w_own.wait()
    w_in.wait_recv()
    rcopy(att.at[1 - core], att.at[1 - core], att_sem.at[0], att_sem.at[1], partner).wait_recv()

    away = pl.multiple_of((1 - yh) * 96, 96)
    home = yh * 96
    first_hops, local_sends = [], []
    for j in range(NJ):
        w0 = wbuf[0:512, j * CW:(j + 1) * CW]
        w1 = wbuf[512:1024, j * CW:(j + 1) * CW]
        part = (jnp.dot(att[0], w0, preferred_element_type=jnp.float32)
                + jnp.dot(att[1], w1, preferred_element_type=jnp.float32))
        pbuf[j] = part.astype(jnp.bfloat16)
        sign = 1 if j % 2 == 0 else -1
        c = rcopy(pbuf.at[j, pl.ds(away, 96)], relay.at[j], rs_send.at[j], rs_recv.at[j], ring_y(sign, core))
        c.start()
        first_hops.append(c)
        c = rcopy(pbuf.at[j, pl.ds(pl.multiple_of(home + 48 * (1 - core), 48), 48)], lbuf.at[j],
                  lo_send.at[j], lo_recv.at[j], partner)
        c.start()
        local_sends.append(c)

    forwards = []
    for j in range(NJ):
        first_hops[j].wait_recv()
        sign = 1 if j % 2 == 0 else -1
        for e in range(2):
            c = rcopy(relay.at[j, pl.ds(48 * e, 48)], rbuf.at[core, j], fw_send.at[2 * j + e],
                      fw_recv.at[core, j], ring_y(sign, e))
            c.start()
            forwards.append(c)

    outs = []
    mine = pl.multiple_of(core * HALF, HALF)
    theirs = pl.multiple_of((1 - core) * HALF, HALF)
    for j in range(NJ):
        rcopy(rbuf.at[core, j], rbuf.at[core, j], fw_send.at[0], fw_recv.at[core, j], partner).wait_recv()
        own = pbuf[j, pl.ds(pl.multiple_of(home + 48 * core, 48), 48), :]
        obuf[core, j] = (own.astype(jnp.float32) + rbuf[core, j].astype(jnp.float32)).astype(jnp.bfloat16)
        c = pltpu.make_async_copy(obuf.at[core, j], out_ref.at[:, pl.ds(mine + j * CW, CW)], out_sem.at[2 * j])
        c.start()
        outs.append(c)
        local_sends[j].wait_recv()
        rcopy(rbuf.at[1 - core, j], rbuf.at[1 - core, j], fw_send.at[0], fw_recv.at[1 - core, j], partner).wait_recv()
        obuf[1 - core, j] = (lbuf[j].astype(jnp.float32) + rbuf[1 - core, j].astype(jnp.float32)).astype(jnp.bfloat16)
        c = pltpu.make_async_copy(obuf.at[1 - core, j], out_ref.at[:, pl.ds(theirs + j * CW, CW)], out_sem.at[2 * j + 1])
        c.start()
        outs.append(c)

    for c in sends + [w_far, att_copy] + first_hops + local_sends + forwards:
        c.wait_send()
    for c in outs:
        c.wait()


N_AG = 65
N_DD = 24


def shards(queries, keys, values, positions, out_weight):
    any_spec = pl.BlockSpec(memory_space=pl.ANY)
    dma = pltpu.SemaphoreType.DMA
    bf, f32 = jnp.bfloat16, jnp.float32
    return pl.pallas_call(
        kernel,
        out_shape=jax.ShapeDtypeStruct((48, NCOL), bf),
        in_specs=[any_spec] * 5,
        out_specs=any_spec,
        scratch_shapes=[
            pltpu.VMEM((3, 2, NCP, 4, 16, HEAD), bf),
            pltpu.VMEM((4, RUN, HEAD), bf),
            pltpu.VMEM((TOK, HEADS * HEAD), bf),
            pltpu.VMEM((2 * HEAD, ROWS), bf),
            pltpu.VMEM((HEAD, ROWS), f32),
            pltpu.VMEM((HEAD, ROWS), f32),
            pltpu.VMEM((8, ROWS), f32),
            pltpu.VMEM((8, ROWS), f32),
            pltpu.VMEM((1, ROWS), f32),
            pltpu.VMEM((1, ROWS), f32),
            pltpu.VMEM((2, TOK, 512), bf),
            pltpu.VMEM((1024, HALF), bf),
            pltpu.VMEM((NJ, TOK, CW), bf),
            pltpu.VMEM((NJ, 96, CW), bf),
            pltpu.VMEM((2, NJ, 48, CW), bf),
            pltpu.VMEM((NJ, 48, CW), bf),
            pltpu.VMEM((2, NJ, 48, CW), bf),
            pltpu.SMEM((NCP * TOK,), jnp.int32),
            dma((16,)),
            dma((2,)),
            dma((3,)),
            dma((N_AG,)),
            dma((N_AG,)),
            dma((N_DD,)),
            dma((N_DD,)),
            dma((2,)),
            dma((NJ,)),
            dma((NJ,)),
            dma((2 * NJ,)),
            dma((2, NJ)),
            dma((NJ,)),
            dma((NJ,)),
            dma((2 * NJ,)),
        ],
        compiler_params=pltpu.CompilerParams(collective_id=0, has_side_effects=True,
                                             vmem_limit_bytes=56 * 1024 * 1024),
    )(queries, keys, values, positions, out_weight)


def solution(mesh):
    in_specs = (P("cp", "tp"), P("cp", None), P("cp", None), P(), P("tp", None))
    out_specs = P(("cp", "tp"), None)
    return jax.shard_map(shards, mesh=mesh, in_specs=in_specs, out_specs=out_specs, check_vma=False)
```

time: 436 us -> 79.2 us (0.18)
  waiting for transfers between devices: 357 us -> 0 us
  Pallas kernels: 0 us -> 77 us
  matrix products: 42.6 us -> 0 us
  other arithmetic: 20.9 us -> 0 us
  between operations: 13.4 us -> 0.01 us
    all_gather x1 -> x0, waiting for transfers between devices: 264 us -> none  [sent_together(): result, at, outs = (lax.all_gather(both, axis, axis=dim, tiled=True), 0, [])]
    reduce_scatter x1 -> x0, waiting for transfers between devices: 92.1 us -> none  [shards(): lax.psum_scatter(jnp.dot(attended, out_weight, preferred_element_type=jnp...]
    pallas_call x0 -> x1, Pallas kernels: none -> 77 us  [shards(): pl.pallas_call(kernel, out_shape=jax.ShapeDtypeStruct((48, NCOL), bf), in...]
    dot_general x3 -> x0, matrix products: 42.6 us -> none  [the longest x1 17.9 us: shards(): jnp.einsum('qhd,kd->qhk', local_queries, arrived_keys, preferred_element_...]
    reduce_sum x1 -> x0, other arithmetic: 18.1 us -> none  [shards(): run_sum = jnp.sum(weights, axis=-1)]
  transfers between devices with their start and end apart: 2 -> 0, of which waited for: 2 -> 0; matrix products, arithmetic and copies ran while one was open for 1% -> 0% of each run, Pallas kernels for 0% -> 0%
where the time goes in v1:
time: 79.2 us; the launch traced here: 79.1 us
  Pallas kernels  77 us (97%)
  local copies, waits for them, and re-layouts  2.06 us (3%)
    pallas_call x1, Pallas kernels, shards(): pl.pallas_call(kernel, out_shape=jax.ShapeDtypeStruct((48, NCOL), bf), in...  77 us
    unnamed x1, local copies, waits for them, and re-layouts  2.06 us

profile of v1, /device:TPU:1, one launch (start us, length us, event | category | flops | bytes accessed | tf_op | source)
XLA Modules:
  0.0 79.1 jit_solution(1080379472447457660)
XLA Ops:
  0.0 77.0 %shard_map.55 = bf16[48,8192]{1,0:T(8,128)(2,1)} custom-call(bf16[192,512]{1,0:T(8,128)(2,1)} %q_ref.1, bf16[192,256]{1,0:T(8,128)(2,1)} %k_ref.1, bf16[192,256]{1,0:T(8,128)(2,1)} %v_ref.1, s32[12288]{0:T(1024)} %pos_ref.1, bf16[512,8192]{1,0:T(8,128)(2,1)} %w_ref.1), custom_call_target="tpu_custom_call" | custom-call | tf_op jit(solution)/shard_map/pallas_call | solution.py:452
  77.0 2.1 %copy.7 = bf16[48,8192]{1,0:T(8,128)(2,1)} copy(bf16[48,8192]{1,0:T(8,128)(2,1)} %shard_map.55) | data formatting | bytes 1572864

commit v2 on v1

v2 whole, which is shorter than its diff:
```python
import functools
import math

import jax
import jax.numpy as jnp
from jax import lax
from jax.experimental import pallas as pl
from jax.experimental.pallas import tpu as pltpu
from jax.sharding import PartitionSpec as P

MESH = pl.DeviceIdType.MESH
HEAD = 128
GROUP = 8
NY, NX, NZ = 2, 4, 8
NCP = NY * NX * NZ
RUN = 96
TOK = 192
HEADS = 4
ROWS = RUN * HEADS
NCOL = 8192
HALF = NCOL // 2
NJ = 8
CW = HALF // NJ
SCALE = HEAD ** (-0.5) * math.log2(math.e)
NEG = -1e30


COPIES = (
    (0, 0, 0, 1, 2, 1), (3, 0, 0, 1, 2, 1), (6, -2, 0, 1, 1, 2), (6, 2, 0, 1, 1, -2), (6, -1, 0, 1, 1, 1),
    (6, 1, 0, 1, 1, -1), (1, 2, 0, 2, 0, 2), (1, -1, 0, 2, 0, 1), (1, 1, 0, 2, 0, -1), (4, -1, 0, 2, 1, 1),
    (4, 1, 0, 2, 1, -1), (5, -1, 0, 2, 0, 1), (5, 1, 0, 2, 0, -1), (6, -4, 0, 1, 1, 2), (6, -3, 0, 1, 1, 1),
    (6, 3, 0, 1, 1, -1), (4, -2, 0, 2, 1, 1), (5, 1, -1, 2, 0, -1), (5, -1, -1, 2, 0, 1), (4, 2, 0, 2, 1, -1),
    (5, 1, 1, 2, 0, -1), (5, -1, 1, 2, 0, 1), (2, -1, 0, 4, 1, 1), (2, 1, 1, 4, 1, -1), (2, 1, 0, 4, 1, -1),
    (2, -1, 1, 4, 1, 1), (5, 2, 0, 2, 0, 1), (7, -1, 0, 8, 0, 1), (7, 1, 0, 8, 0, -1), (8, 0, 0, 8, 2, 1),
    (4, -3, 0, 2, 1, 1), (5, -1, -2, 2, 0, 1), (5, 1, -2, 2, 0, -1), (5, 2, -1, 2, 0, -1), (4, 3, 0, 2, 1, -1),
    (5, -1, 2, 2, 0, 1), (5, 1, 2, 2, 0, -1), (5, 2, 1, 2, 0, -1), (2, -2, 0, 4, 1, 1), (2, 2, 1, 4, 1, -1),
    (2, -2, 1, 4, 1, 1), (2, 2, 0, 4, 1, -1), (7, 2, 1, 4, 0, -1), (8, 1, 0, 8, 2, 1), (4, -4, 0, 2, 1, 1),
    (5, 1, -3, 2, 0, -1), (5, -1, -3, 2, 0, 1), (5, 1, 3, 2, 0, -1), (5, -1, 3, 2, 0, 1), (7, 2, 0, 4, 0, 1),
    (8, -1, 0, 8, 2, 1), (5, 2, -2, 2, 0, 1), (5, 2, 2, 2, 0, 1), (2, -3, 0, 4, 1, 1), (2, 3, 1, 4, 1, -1),
    (2, -3, 1, 4, 1, 1), (2, 3, 0, 4, 1, -1), (5, -1, -4, 2, 0, 1), (5, 1, -4, 2, 0, -1), (5, 2, -3, 2, 0, -1),
    (5, 2, 3, 2, 0, -1), (8, 2, 0, 8, 2, 1), (2, -4, 0, 4, 1, 1), (2, 4, 1, 4, 1, -1), (5, 2, -4, 2, 0, 1),
)
GROUPS = (
    (0, 0, 0), (2, 0, 0), (0, -1, 0), (0, 1, 0), (2, 1, 0), (2, 0, 1), (2, -1, 0), (0, -2, 0), (0, 2, 0), (1, 0, 0),
    (2, 1, 1), (2, 2, 0), (1, -1, 0), (1, 1, 0), (2, -1, 1), (0, -3, 0), (0, 3, 0), (1, 2, 0), (0, -4, 0),
    (2, 2, 1),
)
FIRST = 6
ROUNDS = (
    (0, 0, (0, 106, 107, 108, 1, 109, 110, 111, 112, 4, 5, 2, 113, 114, 3, 115, 8, 9, 116, 117, 118, 10, 119, 120, 121, 12, 15, 7, 6, 122, 123, 124, 125, 200, 14, 11, 126, 13, 127, 128, 129, 201)),
    (1, 0, ()),
    (2, 0, (16, 130, 131, 132, 17, 133, 18, 19, 134, 135, 136, 20, 137, 21, 26, 22, 138, 23, 139, 25, 140, 202, 24, 141, 203, 28, 142, 143, 204, 29, 205, 30, 144, 145, 146, 34, 147, 148, 27, 149, 150, 206, 32)),
    (3, 0, (31, 151, 33)), (4, 0, (35, 152, 36)), (5, 0, (38, 153, 39, 154, 37)), (6, 0, ()),
    (7, 0, (40, 155, 207, 41, 156, 208, 46, 42, 44, 157, 158, 209, 48, 45, 159)),
    (8, 0, (47, 160, 43, 210, 49, 161, 211)), (9, 0, (51,)), (9, 1, (53, 162, 54, 163, 52)),
    (10, 0, (57, 164, 212, 58, 213)), (11, 0, (50, 214, 55, 215, 56, 216, 59)), (12, 0, (60,)), (12, 1, ()),
    (13, 0, ()), (13, 1, ()), (14, 0, (62, 64, 217, 63, 218, 61, 219)), (15, 0, ()), (16, 0, ()), (17, 0, ()),
    (17, 1, ()), (18, 0, ()), (19, 0, ()),
)


def place(copy, x, z, y):
    kind, k0, k1, n = copy[:4]
    at_x, at_z, at_y = (x + k0 + NX) % NX, (z + k0 + NZ) % NZ, 1 - y
    slot = (
        z * 8 + x * 2 + at_y,
        z * 8 + at_x * 2,
        at_z * 8 + k1 * 4,
        x * 16 + z * 2 + at_y,
        x * 16 + at_z * 2,
        at_x * 16 + (z + k1 + NZ) % NZ * 2,
        y * 32 + x * 8 + at_z,
        y * 32 + at_x * 8 + k1 * 4,
        at_y * 32 + at_x * 8,
    )[kind]
    return kind // 3, slot, n


def group_place(group, x, z, y):
    f, k0, k1 = group
    at_x = (x + k0 + NX) % NX
    slot = ((z + k0 + NZ) % NZ * 8, at_x * 16, (y + k1) % 2 * 32 + at_x * 8)[f]
    return f, slot, 16 if f == 1 else 8


def chunk_code(group, half):
    f, k0, k1 = group
    return f * 64 + k0 % 8 * 4 + (k1 if f == 2 else half)


def kernel(q_ref, k_ref, v_ref, pos_ref, w_ref, out_ref,
           kv, own_kv, qv, q2t, acc_l, acc_h, sum_l, sum_h, max_l, max_h,
           s1, s2, p1, p2, vl, v2, top_l, top_h, fade_l, fade_h,
           att, wbuf, pbuf, rbuf, lbuf, obuf, pos, flags,
           fill_sem, in_sem, w_sem, ag_send, ag_recv, dd_send, dd_recv,
           att_sem, rs_send, rs_recv, lo_send, lo_recv, out_sem):
    cp = lax.axis_index("cp")
    tp = lax.axis_index("tp")
    core = tp % 2
    yh = tp // 2
    z = cp % NZ
    x = (cp // NZ) % NX
    y = cp // (NZ * NX)

    def cp_of(yy, xx, zz):
        return (yy * NX + xx) * NZ + zz

    partner = dict(cp=cp, tp=yh * 2 + 1 - core)

    def zz(k):
        return (z + k + NZ) % NZ

    def xx(k):
        return (x + k + NX) % NX

    def at_z(k):
        return dict(cp=cp_of(y, x, zz(k)), tp=tp)

    def at_x(k):
        return dict(cp=cp_of(y, xx(k), z), tp=tp)

    flip = dict(cp=cp_of(1 - y, x, z), tp=tp)
    away_cores = [dict(cp=cp, tp=(1 - yh) * 2 + e) for e in (0, 1)]

    q_copy = pltpu.make_async_copy(q_ref, qv, in_sem.at[0])
    q_copy.start()
    pos_copy = pltpu.make_async_copy(pos_ref, pos, in_sem.at[1])
    pos_copy.start()
    slot_a = z * 8 + x * 2 + y
    slot_b = x * 16 + z * 2 + y
    slot_d = y * 32 + x * 8 + z
    own_slots = (slot_a, slot_b, slot_d)
    fills = []
    cols = pl.ds(pl.multiple_of(yh * HEAD, HEAD), HEAD)
    for f in range(3):
        for h in range(2):
            for src, kind in ((k_ref, 0), (v_ref, 2)):
                rows = pl.ds(pl.multiple_of(h * RUN + 32 * f + 16 * core, 16), 16)
                fills.append(pltpu.make_async_copy(
                    src.at[rows, cols], kv.at[f, core, own_slots[f], kind + h], fill_sem.at[len(fills)]))
    own_fills = []
    for h in range(2):
        for src, kind in ((k_ref, 0), (v_ref, 2)):
            own_fills.append(pltpu.make_async_copy(
                src.at[pl.ds(h * RUN, RUN), cols], own_kv.at[kind + h], fill_sem.at[12 + len(own_fills)]))
    for c in fills + own_fills:
        c.start()

    barrier = pltpu.get_barrier_semaphore()
    peers = [at_z(k) for k in (1, -1, 2, -2)] + [at_x(k) for k in (1, -1, 2)] + [partner, flip] + away_cores
    for p in peers:
        pl.semaphore_signal(barrier, inc=1, device_id=p, device_id_type=MESH)
    pl.semaphore_wait(barrier, len(peers))
    for c in fills:
        c.wait()

    def rcopy(src, dst, ssem, rsem, dev):
        return pltpu.make_async_remote_copy(src_ref=src, dst_ref=dst, send_sem=ssem, recv_sem=rsem,
                                            device_id=dev, device_id_type=MESH)

    def part(owner, where):
        f, slot, n = where
        return kv.at[f, owner, pl.ds(slot, n)]

    def gather(i):
        axis, steps = COPIES[i][4:]
        dev = (at_x, at_z, lambda k: flip)[axis](steps)
        where = place(COPIES[i], xx(steps) if axis == 0 else x, zz(steps) if axis == 1 else z, 1 - y if axis == 2 else y)
        ref = part(core, where)
        return rcopy(ref, ref, ag_send.at[i], ag_recv.at[i], dev)

    def arrive(i):
        ref = part(core, place(COPIES[i], x, z, y))
        return rcopy(ref, ref, ag_send.at[i], ag_recv.at[i], partner)

    def share(i, owner):
        ref = part(owner, group_place(GROUPS[i], x, z, y))
        return rcopy(ref, ref, dd_send.at[i], dd_recv.at[i], partner)

    for i in range(FIRST):
        gather(i).start()

    my_rows = pl.ds(pl.multiple_of(core * 512, 512), 512)
    w_own = pltpu.make_async_copy(
        w_ref.at[:, pl.ds(pl.multiple_of(core * HALF, HALF), HALF)], wbuf.at[my_rows], w_sem.at[0])
    w_own.start()
    w_far = rcopy(w_ref.at[:, pl.ds(pl.multiple_of((1 - core) * HALF, HALF), HALF)], wbuf.at[my_rows],
                  w_sem.at[1], w_sem.at[2], partner)
    w_far.start()
    other_rows = pl.ds(pl.multiple_of((1 - core) * 512, 512), 512)
    w_in = rcopy(w_ref.at[:, pl.ds(0, HALF)], wbuf.at[other_rows], w_sem.at[1], w_sem.at[2], partner)

    q_copy.wait()
    pos_copy.wait()
    own0 = pos[cp * TOK]
    own1 = pos[cp * TOK + RUN]
    own_first = own0 < own1
    own_low = jnp.minimum(own0, own1)

    qa = jnp.concatenate([qv[0:RUN, h * HEAD:(h + 1) * HEAD] for h in range(HEADS)], axis=0)
    qb = jnp.concatenate([qv[RUN:TOK, h * HEAD:(h + 1) * HEAD] for h in range(HEADS)], axis=0)
    q2t[0:HEAD, :] = jnp.where(own_first, qa, qb).T
    q2t[HEAD:2 * HEAD, :] = jnp.where(own_first, qb, qa).T

    TN = (((0,), (0,)), ((), ()))

    for c in own_fills:
        c.wait()

    lane = lax.broadcasted_iota(jnp.int32, (RUN, ROWS), 1)
    keep = lax.broadcasted_iota(jnp.int32, (RUN, ROWS), 0) <= lane % RUN

    def triangle(kk, vv, qt, acc, total, top):
        s = jnp.dot(kk, qt, preferred_element_type=jnp.float32)
        s = jnp.where(keep, s, NEG)
        m = jnp.max(s, axis=0, keepdims=True)
        p = jnp.exp2(s * SCALE - m * SCALE)
        top[...] = m
        total[...] = jnp.sum(p.reshape(RUN // 8, 8, ROWS), axis=0)
        acc[...] = lax.dot_general(vv, p.astype(jnp.bfloat16), TN, preferred_element_type=jnp.float32)

    k0, k1, v0, v1 = (own_kv[i] for i in range(4))
    triangle(jnp.where(own_first, k0, k1), jnp.where(own_first, v0, v1), q2t[0:HEAD, :], acc_l, sum_l, max_l)
    triangle(jnp.where(own_first, k1, k0), jnp.where(own_first, v1, v0), q2t[HEAD:2 * HEAD, :], acc_h, sum_h, max_h)

    zero = jnp.zeros((16, HEAD), jnp.bfloat16)

    cat = functools.partial(jnp.concatenate, axis=0)

    def scores(f, i, r):
        kl, vl_, ka, kb, va, vb, low_f, high_f = ([] for _ in range(8))
        for j in range(8):
            s_z = jnp.where(f == 0, i, jnp.where(f == 1, (i % 2) * 4 + j // 2, j))
            s_x = jnp.where(f == 0, j // 2, jnp.where(f == 1, i // 2, i % 4))
            s_y = jnp.where(f == 2, i // 4, j % 2)
            s = cp_of(s_y, s_x, s_z)
            r0 = pos[s * TOK]
            r1 = pos[s * TOK + RUN]
            first = r0 < r1
            low = jnp.minimum(r0, r1) < own_low
            high = jnp.minimum(r0, r1) > own_low
            low_f.append(low)
            high_f.append(high)
            flags[j] = jnp.where(low, 1, 0)
            flags[8 + j] = jnp.where(high, 1, 0)
            for c in range(2):
                t0, t1, u0, u1 = (kv[f, c, i * 8 + j, n] for n in range(4))
                kl.append(jnp.where(first, t0, t1))
                vl_.append(jnp.where(first, u0, u1))
                ka.append(jnp.where(low, kl[-1], zero))
                va.append(jnp.where(low, vl_[-1], zero))
                kb.append(jnp.where(high, jnp.where(first, t1, t0), zero))
                vb.append(jnp.where(high, jnp.where(first, u1, u0), zero))
        vl[r % 2] = cat(vl_)
        v2[r % 2, :, 0:HEAD] = cat(va)
        v2[r % 2, :, HEAD:2 * HEAD] = cat(vb)
        k2 = jnp.concatenate([cat(ka), cat(kb)], axis=1)
        a = jnp.dot(cat(kl), q2t[HEAD:2 * HEAD, :], preferred_element_type=jnp.float32)
        b = jnp.dot(k2, q2t[...], preferred_element_type=jnp.float32)
        s1[...] = a
        s2[...] = b
        m_h = jnp.max(a.reshape(32, 8, ROWS), axis=0)
        m_l = jnp.full((8, ROWS), NEG, jnp.float32)
        for j in range(8):
            t = jnp.max(b[32 * j:32 * j + 32].reshape(4, 8, ROWS), axis=0)
            m_l = jnp.maximum(m_l, jnp.where(low_f[j], t, NEG))
            m_h = jnp.maximum(m_h, jnp.where(high_f[j], t, NEG))
        top_l[...] = m_l
        top_h[...] = m_h

    def weigh():
        old_l, old_h = max_l[...], max_h[...]
        new_l = jnp.maximum(old_l, jnp.max(top_l[...], axis=0, keepdims=True))
        new_h = jnp.maximum(old_h, jnp.max(top_h[...], axis=0, keepdims=True))
        f_l = jnp.exp2((old_l - new_l) * SCALE)
        f_h = jnp.exp2((old_h - new_h) * SCALE)
        max_l[...] = new_l
        max_h[...] = new_h
        fade_l[...] = f_l
        fade_h[...] = f_h
        at_l = jnp.broadcast_to(new_l * SCALE, (8, ROWS))
        at_h = jnp.broadcast_to(new_h * SCALE, (8, ROWS))
        t_h = sum_h[...] * f_h
        t_l = sum_l[...] * f_l
        for j in range(8):
            rows = slice(32 * j, 32 * j + 32)
            p = jnp.exp2(s1[rows, :].reshape(4, 8, ROWS) * SCALE - at_h[None])
            t_h = t_h + jnp.sum(p, axis=0)
            p1[rows, :] = p.reshape(32, ROWS).astype(jnp.bfloat16)
            low, high = flags[j] > 0, flags[8 + j] > 0
            m = jnp.where(low, at_l, jnp.where(high, at_h, -NEG))
            p = jnp.exp2(s2[rows, :].reshape(4, 8, ROWS) * SCALE - m[None])
            t = jnp.sum(p, axis=0)
            t_l = t_l + jnp.where(low, t, 0.0)
            t_h = t_h + jnp.where(high, t, 0.0)
            p2[rows, :] = p.reshape(32, ROWS).astype(jnp.bfloat16)
        sum_l[...] = t_l
        sum_h[...] = t_h

    def attend(r):
        r1 = lax.dot_general(vl[r % 2], p1[...], TN, preferred_element_type=jnp.float32)
        r2 = lax.dot_general(v2[r % 2], p2[...], TN, preferred_element_type=jnp.float32)
        acc_l[...] = acc_l[...] * fade_l[...] + r2[0:HEAD]
        acc_h[...] = acc_h[...] * fade_h[...] + (r1 + r2[HEAD:2 * HEAD])

    for ref in (s1, s2, top_l, top_h):
        ref[...] = jnp.full(ref.shape, NEG, jnp.float32)
    for ref in (p1, p2, vl, v2):
        ref[...] = jnp.zeros(ref.shape, jnp.bfloat16)
    fade_l[...] = jnp.ones((1, ROWS), jnp.float32)
    fade_h[...] = jnp.ones((1, ROWS), jnp.float32)
    for j in range(16):
        flags[j] = jnp.int32(1)

    met = set()
    codes = [chunk_code(GROUPS[g], half) for g, half, _ in ROUNDS]

    def rounds(r, carry):
        for i, (g, half, events) in enumerate(ROUNDS):
            if not events and g in met:
                continue

            @pl.when(r == i)
            def _():
                for e in events:
                    if e < 100:
                        arrive(e).wait_recv()
                    elif e < 200:
                        gather(e - 100).start()
                    else:
                        share(e - 200, core).start()
                if g not in met:
                    share(g, 1 - core).wait_recv()

            met.add(g)
        code = jnp.int32(0)
        for i, c in enumerate(codes):
            code = jnp.where(r == i, c, code)
        f, k0, k1 = code // 64, code // 4 % 8, code % 4
        i = jnp.where(f == 0, (z + k0) % NZ,
                      jnp.where(f == 1, (x + k0) % NX * 2 + k1, (y + k1) % 2 * 4 + (x + k0) % NX))
        attend(r)
        weigh()
        scores(f, i, r)
        return carry

    lax.fori_loop(0, len(ROUNDS), rounds, 0)
    attend(len(ROUNDS))
    weigh()
    attend(len(ROUNDS) + 1)

    fin_l = acc_l[...] / jnp.sum(sum_l[...], axis=0, keepdims=True)
    fin_h = acc_h[...] / jnp.sum(sum_h[...], axis=0, keepdims=True)
    fin_a = jnp.where(own_first, fin_l, fin_h).T.astype(jnp.bfloat16)
    fin_b = jnp.where(own_first, fin_h, fin_l).T.astype(jnp.bfloat16)
    for h in range(HEADS):
        att[core, 0:RUN, h * HEAD:(h + 1) * HEAD] = fin_a[h * RUN:(h + 1) * RUN]
        att[core, RUN:TOK, h * HEAD:(h + 1) * HEAD] = fin_b[h * RUN:(h + 1) * RUN]
    att_copy = rcopy(att.at[core], att.at[core], att_sem.at[0], att_sem.at[1], partner)
    att_copy.start()
    w_own.wait()
    w_in.wait_recv()
    rcopy(att.at[1 - core], att.at[1 - core], att_sem.at[0], att_sem.at[1], partner).wait_recv()

    home = yh * 96
    far_sends, local_sends = [], []
    for j in range(NJ):
        w0 = wbuf[0:512, j * CW:(j + 1) * CW]
        w1 = wbuf[512:1024, j * CW:(j + 1) * CW]
        product = (jnp.dot(att[0], w0, preferred_element_type=jnp.float32)
                   + jnp.dot(att[1], w1, preferred_element_type=jnp.float32))
        pbuf[j] = product.astype(jnp.bfloat16)
        for e in range(2):
            rows = pl.ds(pl.multiple_of((1 - yh) * 96 + 48 * e, 48), 48)
            c = rcopy(pbuf.at[j, rows], rbuf.at[core, j], rs_send.at[2 * j + e], rs_recv.at[core, j], away_cores[e])
            c.start()
            far_sends.append(c)
        c = rcopy(pbuf.at[j, pl.ds(pl.multiple_of(home + 48 * (1 - core), 48), 48)], lbuf.at[j],
                  lo_send.at[j], lo_recv.at[j], partner)
        c.start()
        local_sends.append(c)

    outs = []
    mine = pl.multiple_of(core * HALF, HALF)
    theirs = pl.multiple_of((1 - core) * HALF, HALF)
    for j in range(NJ):
        rcopy(rbuf.at[core, j], rbuf.at[core, j], rs_send.at[0], rs_recv.at[core, j], partner).wait_recv()
        own = pbuf[j, pl.ds(pl.multiple_of(home + 48 * core, 48), 48), :]
        obuf[core, j] = (own.astype(jnp.float32) + rbuf[core, j].astype(jnp.float32)).astype(jnp.bfloat16)
        c = pltpu.make_async_copy(obuf.at[core, j], out_ref.at[:, pl.ds(mine + j * CW, CW)], out_sem.at[2 * j])
        c.start()
        outs.append(c)
        local_sends[j].wait_recv()
        rcopy(rbuf.at[1 - core, j], rbuf.at[1 - core, j], rs_send.at[0], rs_recv.at[1 - core, j], partner).wait_recv()
        obuf[1 - core, j] = (lbuf[j].astype(jnp.float32) + rbuf[1 - core, j].astype(jnp.float32)).astype(jnp.bfloat16)
        c = pltpu.make_async_copy(obuf.at[1 - core, j], out_ref.at[:, pl.ds(theirs + j * CW, CW)], out_sem.at[2 * j + 1])
        c.start()
        outs.append(c)

    sends = [gather(i) for i in range(len(COPIES))] + [share(i, core) for i in range(len(GROUPS))]
    for c in sends + [w_far, att_copy] + far_sends + local_sends:
        c.wait_send()
    for c in outs:
        c.wait()


def shards(queries, keys, values, positions, out_weight):
    any_spec = pl.BlockSpec(memory_space=pl.ANY)
    dma = pltpu.SemaphoreType.DMA
    bf, f32 = jnp.bfloat16, jnp.float32
    return pl.pallas_call(
        kernel,
        out_shape=jax.ShapeDtypeStruct((48, NCOL), bf),
        in_specs=[any_spec] * 5,
        out_specs=any_spec,
        scratch_shapes=[
            pltpu.VMEM((3, 2, NCP, 4, 16, HEAD), bf),
            pltpu.VMEM((4, RUN, HEAD), bf),
            pltpu.VMEM((TOK, HEADS * HEAD), bf),
            pltpu.VMEM((2 * HEAD, ROWS), bf),
            pltpu.VMEM((HEAD, ROWS), f32),
            pltpu.VMEM((HEAD, ROWS), f32),
            pltpu.VMEM((8, ROWS), f32),
            pltpu.VMEM((8, ROWS), f32),
            pltpu.VMEM((1, ROWS), f32),
            pltpu.VMEM((1, ROWS), f32),
            pltpu.VMEM((256, ROWS), f32),
            pltpu.VMEM((256, ROWS), f32),
            pltpu.VMEM((256, ROWS), bf),
            pltpu.VMEM((256, ROWS), bf),
            pltpu.VMEM((2, 256, HEAD), bf),
            pltpu.VMEM((2, 256, 2 * HEAD), bf),
            pltpu.VMEM((8, ROWS), f32),
            pltpu.VMEM((8, ROWS), f32),
            pltpu.VMEM((1, ROWS), f32),
            pltpu.VMEM((1, ROWS), f32),
            pltpu.VMEM((2, TOK, 512), bf),
            pltpu.VMEM((1024, HALF), bf),
            pltpu.VMEM((NJ, TOK, CW), bf),
            pltpu.VMEM((2, NJ, 48, CW), bf),
            pltpu.VMEM((NJ, 48, CW), bf),
            pltpu.VMEM((2, NJ, 48, CW), bf),
            pltpu.SMEM((NCP * TOK,), jnp.int32),
            pltpu.SMEM((16,), jnp.int32),
            dma((16,)),
            dma((2,)),
            dma((3,)),
            dma((len(COPIES),)),
            dma((len(COPIES),)),
            dma((len(GROUPS),)),
            dma((len(GROUPS),)),
            dma((2,)),
            dma((2 * NJ,)),
            dma((2, NJ)),
            dma((NJ,)),
            dma((NJ,)),
            dma((2 * NJ,)),
        ],
        compiler_params=pltpu.CompilerParams(collective_id=0, has_side_effects=True,
                                             vmem_limit_bytes=56 * 1024 * 1024),
    )(queries, keys, values, positions, out_weight)


def solution(mesh):
    in_specs = (P("cp", "tp"), P("cp", None), P("cp", None), P(), P("tp", None))
    out_specs = P(("cp", "tp"), None)
    return jax.shard_map(shards, mesh=mesh, in_specs=in_specs, out_specs=out_specs, check_vma=False)
```

time: 79.2 us -> 66.6 us (0.84)
  Pallas kernels: 77 us -> 64.4 us
    pallas_call x1, Pallas kernels: 77 us -> 64.4 us  [shards(): pl.pallas_call(kernel, out_shape=jax.ShapeDtypeStruct((48, NCOL), bf), in...]
where the time goes in v2:
time: 66.6 us; the launch traced here: 66.4 us
  Pallas kernels  64.4 us (97%)
  local copies, waits for them, and re-layouts  2.06 us (3%)
    pallas_call x1, Pallas kernels, shards(): pl.pallas_call(kernel, out_shape=jax.ShapeDtypeStruct((48, NCOL), bf), in...  64.4 us
    unnamed x1, local copies, waits for them, and re-layouts  2.06 us

profile of v2, /device:TPU:1, one launch (start us, length us, event | category | flops | bytes accessed | tf_op | source)
XLA Modules:
  0.0 66.4 jit_solution(2154765115499778065)
XLA Ops:
  0.0 64.4 %shard_map.55 = bf16[48,8192]{1,0:T(8,128)(2,1)} custom-call(bf16[192,512]{1,0:T(8,128)(2,1)} %q_ref.1, bf16[192,256]{1,0:T(8,128)(2,1)} %k_ref.1, bf16[192,256]{1,0:T(8,128)(2,1)} %v_ref.1, s32[12288]{0:T(1024)} %pos_ref.1, bf16[512,8192]{1,0:T(8,128)(2,1)} %w_ref.1), custom_call_target="tpu_custom_call" | custom-call | tf_op jit(solution)/shard_map/pallas_call | solution.py:411
  64.4 2.1 %copy.7 = bf16[48,8192]{1,0:T(8,128)(2,1)} copy(bf16[48,8192]{1,0:T(8,128)(2,1)} %shard_map.55) | data formatting | bytes 1572864

commit v3 on v2

--- a/solution.py
+++ b/solution.py
@@ -26,36 +26,36 @@
 
 
 COPIES = (
-    (0, 0, 0, 1, 2, 1), (3, 0, 0, 1, 2, 1), (6, -2, 0, 1, 1, 2), (6, 2, 0, 1, 1, -2), (6, -1, 0, 1, 1, 1),
-    (6, 1, 0, 1, 1, -1), (1, 2, 0, 2, 0, 2), (1, -1, 0, 2, 0, 1), (1, 1, 0, 2, 0, -1), (4, -1, 0, 2, 1, 1),
-    (4, 1, 0, 2, 1, -1), (5, -1, 0, 2, 0, 1), (5, 1, 0, 2, 0, -1), (6, -4, 0, 1, 1, 2), (6, -3, 0, 1, 1, 1),
-    (6, 3, 0, 1, 1, -1), (4, -2, 0, 2, 1, 1), (5, 1, -1, 2, 0, -1), (5, -1, -1, 2, 0, 1), (4, 2, 0, 2, 1, -1),
-    (5, 1, 1, 2, 0, -1), (5, -1, 1, 2, 0, 1), (2, -1, 0, 4, 1, 1), (2, 1, 1, 4, 1, -1), (2, 1, 0, 4, 1, -1),
-    (2, -1, 1, 4, 1, 1), (5, 2, 0, 2, 0, 1), (7, -1, 0, 8, 0, 1), (7, 1, 0, 8, 0, -1), (8, 0, 0, 8, 2, 1),
-    (4, -3, 0, 2, 1, 1), (5, -1, -2, 2, 0, 1), (5, 1, -2, 2, 0, -1), (5, 2, -1, 2, 0, -1), (4, 3, 0, 2, 1, -1),
-    (5, -1, 2, 2, 0, 1), (5, 1, 2, 2, 0, -1), (5, 2, 1, 2, 0, -1), (2, -2, 0, 4, 1, 1), (2, 2, 1, 4, 1, -1),
-    (2, -2, 1, 4, 1, 1), (2, 2, 0, 4, 1, -1), (7, 2, 1, 4, 0, -1), (8, 1, 0, 8, 2, 1), (4, -4, 0, 2, 1, 1),
-    (5, 1, -3, 2, 0, -1), (5, -1, -3, 2, 0, 1), (5, 1, 3, 2, 0, -1), (5, -1, 3, 2, 0, 1), (7, 2, 0, 4, 0, 1),
-    (8, -1, 0, 8, 2, 1), (5, 2, -2, 2, 0, 1), (5, 2, 2, 2, 0, 1), (2, -3, 0, 4, 1, 1), (2, 3, 1, 4, 1, -1),
-    (2, -3, 1, 4, 1, 1), (2, 3, 0, 4, 1, -1), (5, -1, -4, 2, 0, 1), (5, 1, -4, 2, 0, -1), (5, 2, -3, 2, 0, -1),
-    (5, 2, 3, 2, 0, -1), (8, 2, 0, 8, 2, 1), (2, -4, 0, 4, 1, 1), (2, 4, 1, 4, 1, -1), (5, 2, -4, 2, 0, 1),
+    (0, 0, 0, 1, 2, 1), (6, -2, 0, 1, 1, 2), (6, 2, 0, 1, 1, -2), (3, 0, 0, 1, 2, 1), (6, -1, 0, 1, 1, 1),
+    (6, 1, 0, 1, 1, -1), (1, 2, 0, 2, 0, 2), (1, -1, 0, 2, 0, 1), (1, 1, 0, 2, 0, -1), (4, -2, 0, 2, 1, 2),
+    (4, 2, 0, 2, 1, -2), (4, -1, 0, 2, 1, 1), (4, 1, 0, 2, 1, -1), (5, -1, 0, 2, 0, 1), (5, 1, 0, 2, 0, -1),
+    (6, -4, 0, 1, 1, 2), (6, -3, 0, 1, 1, 1), (6, 3, 0, 1, 1, -1), (2, -1, 0, 4, 1, 1), (2, 1, 1, 4, 1, -1),
+    (2, 1, 0, 4, 1, -1), (2, -1, 1, 4, 1, 1), (5, 1, -1, 2, 0, -1), (5, -1, -1, 2, 0, 1), (5, 1, 1, 2, 0, -1),
+    (5, -1, 1, 2, 0, 1), (4, -4, 0, 2, 1, 2), (4, -3, 0, 2, 1, 1), (5, -1, -2, 2, 0, 1), (5, 1, -2, 2, 0, -1),
+    (4, 3, 0, 2, 1, -1), (5, -1, 2, 2, 0, 1), (5, 1, 2, 2, 0, -1), (5, 2, 0, 2, 0, 1), (7, -1, 0, 8, 0, 1),
+    (7, 1, 0, 8, 0, -1), (8, 0, 0, 8, 2, 1), (5, 2, -1, 2, 0, -1), (2, -2, 0, 4, 1, 1), (2, 2, 1, 4, 1, -1),
+    (5, 2, 1, 2, 0, -1), (5, 2, -2, 2, 0, 1), (2, -2, 1, 4, 1, 1), (2, 2, 0, 4, 1, -1), (5, 2, 2, 2, 0, 1),
+    (5, 1, 3, 2, 0, -1), (5, -1, 3, 2, 0, 1), (5, 1, -3, 2, 0, -1), (5, -1, -3, 2, 0, 1), (5, -1, -4, 2, 0, 1),
+    (5, 1, -4, 2, 0, -1), (7, 2, 1, 4, 0, -1), (8, 1, 0, 8, 2, 1), (7, 2, 0, 4, 0, 1), (8, -1, 0, 8, 2, 1),
+    (2, -3, 0, 4, 1, 1), (2, 3, 1, 4, 1, -1), (2, -3, 1, 4, 1, 1), (5, 2, 3, 2, 0, -1), (2, 3, 0, 4, 1, -1),
+    (5, 2, -3, 2, 0, -1), (5, 2, -4, 2, 0, 1), (8, 2, 0, 8, 2, 1), (2, -4, 0, 4, 1, 1), (2, 4, 1, 4, 1, -1),
 )
 GROUPS = (
-    (0, 0, 0), (2, 0, 0), (0, -1, 0), (0, 1, 0), (2, 1, 0), (2, 0, 1), (2, -1, 0), (0, -2, 0), (0, 2, 0), (1, 0, 0),
-    (2, 1, 1), (2, 2, 0), (1, -1, 0), (1, 1, 0), (2, -1, 1), (0, -3, 0), (0, 3, 0), (1, 2, 0), (0, -4, 0),
+    (0, 0, 0), (2, 0, 0), (0, -1, 0), (0, 1, 0), (2, 0, 1), (1, 0, 0), (2, 1, 0), (2, -1, 0), (0, -2, 0), (0, 2, 0),
+    (1, 1, 0), (1, -1, 0), (2, 2, 0), (2, 1, 1), (0, -3, 0), (0, 3, 0), (1, 2, 0), (2, -1, 1), (0, -4, 0),
     (2, 2, 1),
 )
 FIRST = 6
 ROUNDS = (
-    (0, 0, (0, 106, 107, 108, 1, 109, 110, 111, 112, 4, 5, 2, 113, 114, 3, 115, 8, 9, 116, 117, 118, 10, 119, 120, 121, 12, 15, 7, 6, 122, 123, 124, 125, 200, 14, 11, 126, 13, 127, 128, 129, 201)),
+    (0, 0, (0, 106, 107, 108, 3, 109, 110, 111, 112, 113, 114, 4, 5, 1, 115, 116, 2, 117, 8, 14, 7, 6, 118, 119, 120, 121, 200, 11, 122, 123, 12, 124, 125, 9, 126, 127, 128, 129, 10, 130, 131, 132, 13, 133, 17, 16, 15, 134, 135, 136, 201)),
     (1, 0, ()),
-    (2, 0, (16, 130, 131, 132, 17, 133, 18, 19, 134, 135, 136, 20, 137, 21, 26, 22, 138, 23, 139, 25, 140, 202, 24, 141, 203, 28, 142, 143, 204, 29, 205, 30, 144, 145, 146, 34, 147, 148, 27, 149, 150, 206, 32)),
-    (3, 0, (31, 151, 33)), (4, 0, (35, 152, 36)), (5, 0, (38, 153, 39, 154, 37)), (6, 0, ()),
-    (7, 0, (40, 155, 207, 41, 156, 208, 46, 42, 44, 157, 158, 209, 48, 45, 159)),
-    (8, 0, (47, 160, 43, 210, 49, 161, 211)), (9, 0, (51,)), (9, 1, (53, 162, 54, 163, 52)),
-    (10, 0, (57, 164, 212, 58, 213)), (11, 0, (50, 214, 55, 215, 56, 216, 59)), (12, 0, (60,)), (12, 1, ()),
-    (13, 0, ()), (13, 1, ()), (14, 0, (62, 64, 217, 63, 218, 61, 219)), (15, 0, ()), (16, 0, ()), (17, 0, ()),
-    (17, 1, ()), (18, 0, ()), (19, 0, ()),
+    (2, 0, (22, 137, 23, 18, 138, 19, 139, 24, 140, 25, 29, 28, 141, 21, 142, 202, 20, 143, 203, 32, 31, 144, 30, 145, 146, 33)),
+    (3, 0, (36, 204, 27, 147, 148, 26, 149, 150, 205)),
+    (4, 0, (35, 151, 152, 206, 37, 34, 153, 154, 207, 38, 155, 39, 156)), (5, 0, (40, 41)),
+    (5, 1, (44, 42, 157, 208, 45, 158, 43, 159, 209, 46)), (6, 0, ()), (7, 0, (47, 160, 48)),
+    (8, 0, (50, 210, 49, 161, 211)), (9, 0, ()), (10, 0, (51, 53, 162, 212, 55, 163, 56, 164)),
+    (10, 1, (52, 213, 58)), (11, 0, (57, 214, 59, 215)), (11, 1, (60,)), (12, 0, (61, 216)), (13, 0, (54, 217)),
+    (14, 0, ()), (15, 0, ()), (16, 0, (63, 64, 218)), (16, 1, ()), (17, 0, (62, 219)), (18, 0, ()), (19, 0, ()),
 )
 
 
@@ -91,9 +91,9 @@
 def kernel(q_ref, k_ref, v_ref, pos_ref, w_ref, out_ref,
            kv, own_kv, qv, q2t, acc_l, acc_h, sum_l, sum_h, max_l, max_h,
            s1, s2, p1, p2, vl, v2, top_l, top_h, fade_l, fade_h,
-           att, wbuf, pbuf, rbuf, lbuf, obuf, pos, flags,
+           att, wbuf, pbuf, rbuf, lbuf, pos, flags,
            fill_sem, in_sem, w_sem, ag_send, ag_recv, dd_send, dd_recv,
-           att_sem, rs_send, rs_recv, lo_send, lo_recv, out_sem):
+           att_sem, rs_send, rs_recv, lo_send, lo_recv):
     cp = lax.axis_index("cp")
     tp = lax.axis_index("tp")
     core = tp % 2
@@ -147,7 +147,9 @@
         c.start()
 
     barrier = pltpu.get_barrier_semaphore()
-    peers = [at_z(k) for k in (1, -1, 2, -2)] + [at_x(k) for k in (1, -1, 2)] + [partner, flip] + away_cores
+    x_steps = sorted({sign * c[5] % NX for c in COPIES if c[4] == 0 for sign in (1, -1)})
+    z_steps = sorted({sign * c[5] % NZ for c in COPIES if c[4] == 1 for sign in (1, -1)})
+    peers = [at_z(k) for k in z_steps] + [at_x(k) for k in x_steps] + [partner, flip] + away_cores
     for p in peers:
         pl.semaphore_signal(barrier, inc=1, device_id=p, device_id_type=MESH)
     pl.semaphore_wait(barrier, len(peers))
@@ -312,30 +314,33 @@
     for j in range(16):
         flags[j] = jnp.int32(1)
 
-    met = set()
     codes = [chunk_code(GROUPS[g], half) for g, half, _ in ROUNDS]
+    words = [codes[i] + 256 * codes[i + 1] + 65536 * codes[i + 2] for i in range(0, len(codes), 3)]
+
+    def events_of(lo, hi, r):
+        if hi - lo > 1:
+            mid = (lo + hi) // 2
+            pl.when(r < mid)(lambda: events_of(lo, mid, r))
+            pl.when(r >= mid)(lambda: events_of(mid, hi, r))
+            return
+        g, _, events = ROUNDS[lo]
+        for e in events:
+            if e < 100:
+                arrive(e).wait_recv()
+            elif e < 200:
+                gather(e - 100).start()
+            else:
+                share(e - 200, core).start()
+        if g not in [other[0] for other in ROUNDS[:lo]]:
+            share(g, 1 - core).wait_recv()
 
     def rounds(r, carry):
-        for i, (g, half, events) in enumerate(ROUNDS):
-            if not events and g in met:
-                continue
-
-            @pl.when(r == i)
-            def _():
-                for e in events:
-                    if e < 100:
-                        arrive(e).wait_recv()
-                    elif e < 200:
-                        gather(e - 100).start()
-                    else:
-                        share(e - 200, core).start()
-                if g not in met:
-                    share(g, 1 - core).wait_recv()
-
-            met.add(g)
-        code = jnp.int32(0)
-        for i, c in enumerate(codes):
-            code = jnp.where(r == i, c, code)
+        events_of(0, len(ROUNDS), r)
+        third = r // 3
+        word = jnp.int32(0)
+        for i, c in enumerate(words):
+            word = jnp.where(third == i, c, word)
+        code = jnp.where(r % 3 == 0, word % 256, jnp.where(r % 3 == 1, word // 256 % 256, word // 65536))
         f, k0, k1 = code // 64, code // 4 % 8, code % 4
         i = jnp.where(f == 0, (z + k0) % NZ,
                       jnp.where(f == 1, (x + k0) % NX * 2 + k1, (y + k1) % 2 * 4 + (x + k0) % NX))
@@ -380,39 +385,31 @@
         c.start()
         local_sends.append(c)
 
-    outs = []
     mine = pl.multiple_of(core * HALF, HALF)
     theirs = pl.multiple_of((1 - core) * HALF, HALF)
     for j in range(NJ):
         rcopy(rbuf.at[core, j], rbuf.at[core, j], rs_send.at[0], rs_recv.at[core, j], partner).wait_recv()
         own = pbuf[j, pl.ds(pl.multiple_of(home + 48 * core, 48), 48), :]
-        obuf[core, j] = (own.astype(jnp.float32) + rbuf[core, j].astype(jnp.float32)).astype(jnp.bfloat16)
-        c = pltpu.make_async_copy(obuf.at[core, j], out_ref.at[:, pl.ds(mine + j * CW, CW)], out_sem.at[2 * j])
-        c.start()
-        outs.append(c)
+        out_ref[:, pl.ds(mine + j * CW, CW)] = (
+            own.astype(jnp.float32) + rbuf[core, j].astype(jnp.float32)).astype(jnp.bfloat16)
         local_sends[j].wait_recv()
         rcopy(rbuf.at[1 - core, j], rbuf.at[1 - core, j], rs_send.at[0], rs_recv.at[1 - core, j], partner).wait_recv()
-        obuf[1 - core, j] = (lbuf[j].astype(jnp.float32) + rbuf[1 - core, j].astype(jnp.float32)).astype(jnp.bfloat16)
-        c = pltpu.make_async_copy(obuf.at[1 - core, j], out_ref.at[:, pl.ds(theirs + j * CW, CW)], out_sem.at[2 * j + 1])
-        c.start()
-        outs.append(c)
+        out_ref[:, pl.ds(theirs + j * CW, CW)] = (
+            lbuf[j].astype(jnp.float32) + rbuf[1 - core, j].astype(jnp.float32)).astype(jnp.bfloat16)
 
     sends = [gather(i) for i in range(len(COPIES))] + [share(i, core) for i in range(len(GROUPS))]
     for c in sends + [w_far, att_copy] + far_sends + local_sends:
         c.wait_send()
-    for c in outs:
-        c.wait()
 
 
 def shards(queries, keys, values, positions, out_weight):
-    any_spec = pl.BlockSpec(memory_space=pl.ANY)
     dma = pltpu.SemaphoreType.DMA
     bf, f32 = jnp.bfloat16, jnp.float32
     return pl.pallas_call(
         kernel,
         out_shape=jax.ShapeDtypeStruct((48, NCOL), bf),
-        in_specs=[any_spec] * 5,
-        out_specs=any_spec,
+        in_specs=[pl.BlockSpec(memory_space=pltpu.HBM)] * 5,
+        out_specs=pl.BlockSpec(memory_space=pltpu.VMEM),
         scratch_shapes=[
             pltpu.VMEM((3, 2, NCP, 4, 16, HEAD), bf),
             pltpu.VMEM((4, RUN, HEAD), bf),
@@ -439,7 +436,6 @@
             pltpu.VMEM((NJ, TOK, CW), bf),
             pltpu.VMEM((2, NJ, 48, CW), bf),
             pltpu.VMEM((NJ, 48, CW), bf),
-            pltpu.VMEM((2, NJ, 48, CW), bf),
             pltpu.SMEM((NCP * TOK,), jnp.int32),
             pltpu.SMEM((16,), jnp.int32),
             dma((16,)),
@@ -454,11 +450,10 @@
             dma((2, NJ)),
             dma((NJ,)),
             dma((NJ,)),
-            dma((2 * NJ,)),
         ],
         compiler_params=pltpu.CompilerParams(collective_id=0, has_side_effects=True,
-                                             vmem_limit_bytes=56 * 1024 * 1024),
-    )(queries, keys, values, positions, out_weight)
+                                             vmem_limit_bytes=48 * 1024 * 1024),
+    )(*(pltpu.with_memory_space_constraint(a, pltpu.HBM) for a in (queries, keys, values, positions)), out_weight)
 
 
 def solution(mesh):

time: 66.6 us -> 61.6 us (0.925)
  Pallas kernels: 64.4 us -> 60.6 us
  local copies, waits for them, and re-layouts: 2.06 us -> 0.88 us
    pallas_call x1, Pallas kernels: 64.4 us -> 60.6 us  [shards(): pl.pallas_call(kernel, out_shape=jax.ShapeDtypeStruct((48, NCOL), bf), in...]
    unnamed x1, local copies, waits for them, and re-layouts: 2.06 us -> 0.88 us
where the time goes in v3:
time: 61.6 us; the launch traced here: 61.5 us
  Pallas kernels  60.6 us (98%)
  local copies, waits for them, and re-layouts  0.88 us (1%)
    pallas_call x1, Pallas kernels, shards(): pl.pallas_call(kernel, out_shape=jax.ShapeDtypeStruct((48, NCOL), bf), in...  60.6 us

profile of v3, /device:TPU:1, one launch (start us, length us, event | category | flops | bytes accessed | tf_op | source)
XLA Modules:
  0.0 61.5 jit_solution(3607650283245952106)
XLA Ops:
  0.0 60.6 %shard_map.55 = bf16[48,8192]{1,0:T(8,128)(2,1)S(1)} custom-call(bf16[192,512]{1,0:T(8,128)(2,1)} %q_ref.1, bf16[192,256]{1,0:T(8,128)(2,1)} %k_ref.1, bf16[192,256]{1,0:T(8,128)(2,1)} %v_ref.1, s32[12288]{0:T(1024)} %pos_ref.1, bf16[512,8192]{1,0:T(8,128)(2,1)} %w_ref.1), custom_call_target="tpu_custom_call" | custom-call | tf_op jit(solution)/shard_map/pallas_call | solution.py:408
  60.6 0.9 %copy.7 = bf16[48,8192]{1,0:T(8,128)(2,1)} copy(bf16[48,8192]{1,0:T(8,128)(2,1)S(1)} %shard_map.55) | data formatting | bytes 1572864

commit v4 on v3

--- a/solution.py
+++ b/solution.py
@@ -146,6 +146,11 @@
     for c in fills + own_fills:
         c.start()
 
+    my_rows = pl.ds(pl.multiple_of(core * 512, 512), 512)
+    w_own = pltpu.make_async_copy(
+        w_ref.at[:, pl.ds(pl.multiple_of(core * HALF, HALF), HALF)], wbuf.at[my_rows], w_sem.at[0])
+    w_own.start()
+
     barrier = pltpu.get_barrier_semaphore()
     x_steps = sorted({sign * c[5] % NX for c in COPIES if c[4] == 0 for sign in (1, -1)})
     z_steps = sorted({sign * c[5] % NZ for c in COPIES if c[4] == 1 for sign in (1, -1)})
@@ -182,10 +187,6 @@
     for i in range(FIRST):
         gather(i).start()
 
-    my_rows = pl.ds(pl.multiple_of(core * 512, 512), 512)
-    w_own = pltpu.make_async_copy(
-        w_ref.at[:, pl.ds(pl.multiple_of(core * HALF, HALF), HALF)], wbuf.at[my_rows], w_sem.at[0])
-    w_own.start()
     w_far = rcopy(w_ref.at[:, pl.ds(pl.multiple_of((1 - core) * HALF, HALF), HALF)], wbuf.at[my_rows],
                   w_sem.at[1], w_sem.at[2], partner)
     w_far.start()

time: 61.6 us -> 61.6 us (level)
  no operation moved by 1% of the time
where the time goes in v4:
time: 61.6 us; the launch traced here: 61.5 us
  Pallas kernels  60.6 us (98%)
  local copies, waits for them, and re-layouts  0.88 us (1%)
    pallas_call x1, Pallas kernels, shards(): pl.pallas_call(kernel, out_shape=jax.ShapeDtypeStruct((48, NCOL), bf), in...  60.6 us

profile of v4, /device:TPU:1, one launch (start us, length us, event | category | flops | bytes accessed | tf_op | source)
XLA Modules:
  0.0 61.5 jit_solution(8363954159125510857)
XLA Ops:
  0.0 60.6 %shard_map.55 = bf16[48,8192]{1,0:T(8,128)(2,1)S(1)} custom-call(bf16[192,512]{1,0:T(8,128)(2,1)} %q_ref.1, bf16[192,256]{1,0:T(8,128)(2,1)} %k_ref.1, bf16[192,256]{1,0:T(8,128)(2,1)} %v_ref.1, s32[12288]{0:T(1024)} %pos_ref.1, bf16[512,8192]{1,0:T(8,128)(2,1)} %w_ref.1), custom_call_target="tpu_custom_call" | custom-call | tf_op jit(solution)/shard_map/pallas_call | solution.py:409
  60.6 0.9 %copy.7 = bf16[48,8192]{1,0:T(8,128)(2,1)} copy(bf16[48,8192]{1,0:T(8,128)(2,1)S(1)} %shard_map.55) | data formatting | bytes 1572864
